TPU v7x, 32 devices: a whole 2x2x4 slice. The times are simulated.
32 devices in a mesh: dp: 4 (over y, core), vocab: 8 (over z, x).
Axes of the slice: x: 2, y: 2, z: 4, core: 2. Of those that a mesh axis runs over, the one named last changes fastest.
Arguments:
- student_hidden: bfloat16 [512, 2048], P('dp', 'vocab'), may hold values from -210 to 210
- student_blocks: bfloat16 [8, 1024, 4864], P('vocab', 'dp'), may hold values from -0.375 to 0.375
- teacher_logits: bfloat16 [512, 19456], P('dp', 'vocab'), may hold values from -16 to 308
- token_ids: int32 [512], P('dp'), may hold values from 0 to 19455
- loss_mask: int32 [512], P('dp'), may hold values from 0 to 1, as said below
Outputs:
- hidden_grad: bfloat16 [512, 2048], P('dp', 'vocab')
- token_kl: float32 [512], P('dp')
- sampled_logprob: float32 [512], P('dp')
- loss: float32 [], replicated
Inputs may be any that keep to these rules, and one draw needn't show every extreme that they name: `loss_mask`: in each block of 128 tokens the mask is 0 on a leading run of at most 64 tokens and 1 on the rest.
All inputs are finite; a program needn't handle non-finite values.
Results may differ from a plain program's by a relative error of at most 0.0047.
Values may be sent and summed in bfloat16 or wider, within the bound.
No kernel may reach another device: no remote copies, remote signals or barrier semaphores. Data moves between devices by JAX's collectives and lax.ppermute only.
A program may use at most 64 MiB of HBM per device.

v0:
```python
import jax
import jax.numpy as jnp
from jax import lax
from jax.sharding import PartitionSpec as P

D = 2048
VT = 2432


def swapped(shard, axis, stride):
    return lax.ppermute(shard, axis, [(i, i ^ 1 << stride) for i in range(lax.axis_size(axis))])


def combined_all(part, axis, combine):
    gathered = jax.tree.map(lambda a: lax.all_gather(a, axis), part)

    def take(source):
        return jax.tree.map(lambda a: lax.dynamic_index_in_dim(a, source, 0, False), gathered)

    return lax.fori_loop(
        1, lax.axis_size(axis), lambda source, state: combine(state, take(source)), take(0)
    )


def pair_merge(left_pair, right_pair):
    left_max, left_total = left_pair
    right_max, right_total = right_pair
    top_value = jnp.maximum(left_max, right_max)
    merged_total = left_total * jnp.exp(left_max - top_value) + right_total * jnp.exp(
        right_max - top_value
    )
    return (top_value, merged_total)


def row_stats(values):
    row_max = jnp.max(values, axis=1)
    row_total = jnp.sum(jnp.exp(values - row_max[:, None]), axis=1)
    return (row_max, row_total)


def on_device(student_hidden, student_blocks, teacher_logits, token_ids, loss_mask):
    vocab_index = lax.axis_index("vocab")
    pair_side = vocab_index % 2
    mask_float = loss_mask.astype(jnp.float32)
    mask_total = lax.psum(jnp.sum(mask_float), "dp")
    gathered = lax.all_gather(student_hidden, "vocab", axis=1, tiled=True)
    piece = student_blocks[0]
    own_block = lax.dynamic_slice_in_dim(piece, pair_side * VT, VT, 1)
    far_block = lax.dynamic_slice_in_dim(piece, (1 - pair_side) * VT, VT, 1)
    received = swapped(far_block, "vocab", 0)
    stacked = jnp.where(
        pair_side == 0, jnp.stack([own_block, received]), jnp.stack([received, own_block])
    )
    weight = lax.all_gather(stacked, "dp", axis=1, tiled=True).reshape(D, VT)
    logits = jnp.dot(gathered, weight, preferred_element_type=jnp.float32)
    column_start = vocab_index * VT
    teacher_local = teacher_logits.astype(jnp.float32)
    teacher_full = teacher_logits.astype(jnp.float32)
    teacher_max = lax.pmax(jnp.max(teacher_full, axis=1), "vocab")
    teacher_total = lax.psum(jnp.sum(jnp.exp(teacher_full - teacher_max[:, None]), axis=1), "vocab")
    student_max, student_total = row_stats(logits)
    merged = combined_all((student_max, student_total), "vocab", pair_merge)
    stats = (teacher_max, teacher_total, merged[0], merged[1])
    teacher_logp = teacher_local - stats[0][:, None] - jnp.log(stats[1])[:, None]
    student_logp = logits - stats[2][:, None] - jnp.log(stats[3])[:, None]
    teacher_prob = jnp.exp(teacher_logp)
    kl_part = jnp.sum(teacher_prob * (teacher_logp - student_logp), axis=1)
    columns = lax.broadcasted_iota(jnp.int32, logits.shape, 1) + column_start
    sampled_part = jnp.sum(jnp.where(columns == token_ids[:, None], student_logp, 0.0), axis=1)
    token_kl, sampled = lax.psum((kl_part, sampled_part), "vocab")
    loss = lax.psum(jnp.sum(mask_float * token_kl), "dp") / mask_total
    factor = mask_float / mask_total
    dlogits = (factor[:, None] * (jnp.exp(student_logp) - teacher_prob)).astype(jnp.bfloat16)
    term = lax.dot_general(
        dlogits, weight, (((1,), (1,)), ((), ())), preferred_element_type=jnp.float32
    )
    hidden_grad = lax.psum_scatter(term, "vocab", scatter_dimension=1, tiled=True).astype(
        jnp.bfloat16
    )
    return (hidden_grad, token_kl, sampled, loss)


def solution(mesh):
    return jax.shard_map(
        on_device,
        mesh=mesh,
        in_specs=(P("dp", "vocab"), P("vocab", "dp", None), P("dp", "vocab"), P("dp"), P("dp")),
        out_specs=(P("dp", "vocab"), P("dp"), P("dp"), P()),
        check_vma=False,
    )
```

profile of v0, /device:TPU:0, one launch (start us, length us, event | category | flops | bytes accessed | tf_op | source)
XLA Modules:
  0.0 265.2 jit_solution(2844016320098941567)
XLA Ops:
  7.2 0.0 all-gather.6.cloned.1.call-start
  7.2 2.9 %constant_dynamic-slice_fusion.1 = (bf16[1,256,2432]{2,1,0:T(8,128)(2,1)S(1)}, bf16[256,2432]{1,0:T(8,128)(2,1)}) fusion(bf16[1,256,4864]{2,1,0:T(8,128)(2,1)} %param.8, s32[]{:T(128)S(6)} %select_n.41, s32[]{:T(128)S(6)} %select_n.42), kind=kLoop, calls=%fused_computation.33 | loop fusion | bytes 4980744 | tf_op jit(solution)/shard_map/dynamic_slice | solution.py:48
  10.1 3.0 %collective-permute-start = (bf16[256,2432]{1,0:T(8,128)(2,1)}, bf16[256,2432]{1,0:T(8,128)(2,1)S(1)}, u32[]{:S(2)}, u32[]{:S(2)}) collective-permute-start(bf16[256,2432]{1,0:T(8,128)(2,1)} %get-tuple-element.160), channel_id=1, source_target_pairs={{0,1},{1,0},{2,3},{3,2},{4,5},{5,4},{6,7},{7,6},{8,9},{9,8},{10,11... | collective-permute-start | bytes 3735560 | tf_op jit(solution)/shard_map/ppermute | solution.py:11
  13.1 27.6 %collective-permute-done = bf16[256,2432]{1,0:T(8,128)(2,1)S(1)} collective-permute-done((bf16[256,2432]{1,0:T(8,128)(2,1)}, bf16[256,2432]{1,0:T(8,128)(2,1)S(1)}, u32[]{:S(2)}, u32[]{:S(2)}) %collective-permute-start) | collective-permute-done | bytes 1245216 | tf_op jit(solution)/shard_map/ppermute | solution.py:11
  40.7 1.8 maximum_select_fusion
  42.5 0.0 copy-start
  42.5 0.0 all-gather.6.cloned.1.call-update
  42.5 0.0 reduce-scatter.2.cloned.1.call-start
  42.6 1.0 copy-done
  43.6 0.0 copy-start.1
  43.6 0.3 copy.10
  43.9 0.2 reduce_max.24
  44.1 21.9 %pmax.7 = f32[128]{0:T(128)S(1)} all-reduce(bf16[128]{0:T(256)(128)(2,1)S(1)} %reduce_max.24), channel_id=1, replica_groups=mesh['dp'=4,'vocab'=8] {'vocab'}, use_global_device_ids=true, to_apply=%region_7.8 | all-reduce | flops 128 | bytes 768 | tf_op jit(solution)/shard_map/pmax | solution.py:59
  66.0 0.3 exponential_reduce_fusion
  66.3 17.1 %psum.36 = f32[128]{0:T(128)S(1)} all-reduce(f32[128]{0:T(128)S(1)} %exponential_reduce_fusion), channel_id=1, replica_groups=mesh['dp'=4,'vocab'=8] {'vocab'}, use_global_device_ids=true, to_apply=%region_9.10 | all-reduce | flops 128 | bytes 1024 | tf_op jit(solution)/shard_map/psum | solution.py:60
  83.5 0.0 copy-done.1
  83.5 31.2 %all_gather.19 = bf16[128,2048]{1,0:T(8,128)(2,1)S(1)} all-gather(bf16[128,256]{1,0:T(8,128)(2,1)S(1)} %copy-done.1), channel_id=1, replica_groups=mesh['dp'=4,'vocab'=8] {'vocab'}, dimensions={1}, use_global_device_ids=true | all-gather | bytes 589824 | tf_op jit(solution)/shard_map/all_gather | solution.py:46
  114.7 0.0 all-gather.6.cloned.1.call-done
  114.7 6.6 %fusion.17 = (f32[128]{0:T(128)S(1)}, f32[2432,128]{1,0:T(8,128)S(1)}) fusion(bf16[2048,2432]{1,0:T(8,128)(2,1)} %bitcast.46, bf16[128,2048]{1,0:T(8,128)(2,1)S(1)} %all_gather.19), kind=kOutput, calls=%fused_computation.36 | convolution fusion | flops 1275379584 | bytes 11731456 | tf_op jit(solution)/shard_map/dot_general | solution.py:55
  121.4 0.0 copy-start.2
  121.4 0.3 exponential_reduce_fusion.1
  121.7 0.0 copy-start.3
  121.7 18.5 %all-gather.3 = f32[8,1,128]{2,1,0:T(1,128)S(1)} all-gather(f32[1,1,128]{2,1,0:T(1,128)S(1)} %bitcast.52), channel_id=3, replica_groups=mesh['dp'=4,'vocab'=8] {'vocab'}, dimensions={0}, use_global_device_ids=true | all-gather | bytes 4608 | tf_op jit(solution)/shard_map/all_gather | solution.py:15
  140.2 16.3 %all-gather.2 = f32[8,1,128]{2,1,0:T(1,128)S(1)} all-gather(f32[1,1,128]{2,1,0:T(1,128)S(1)} %bitcast.51), channel_id=2, replica_groups=mesh['dp'=4,'vocab'=8] {'vocab'}, dimensions={0}, use_global_device_ids=true | all-gather | bytes 4608 | tf_op jit(solution)/shard_map/all_gather | solution.py:15
  156.5 0.3 while.17
  156.8 0.0 copy-done.2
  156.8 1.1 fusion.7
  157.9 19.7 %all-reduce = (f32[128]{0:T(128)S(1)}, f32[128]{0:T(128)}) all-reduce(f32[128]{0:T(128)S(1)} %get-tuple-element.140, f32[128]{0:T(128)S(1)} %get-tuple-element.139), channel_id=1, replica_groups=mesh['dp'=4,'vocab'=8] {'vocab'}, use_global_device_ids=true, to_apply=%region_12.13 | all-reduce | flops 256 | bytes 2048 | tf_op jit(solution)/shard_map/psum | solution.py:70
  177.6 0.0 copy-start.4
  177.6 0.0 copy-done.3
  177.6 0.6 multiply_reduce_fusion
  178.2 6.3 %all-reduce.1 = (f32[]{:T(128)}, f32[]{:T(128)}) all-reduce(f32[]{:T(128)} %get-tuple-element.142, f32[]{:T(128)} %get-tuple-element.141), channel_id=1, replica_groups=mesh['dp'=4,'vocab'=8] {'dp'}, use_global_device_ids=true, to_apply=%region_1.2 | all-reduce | flops 2 | bytes 16 | tf_op jit(solution)/shard_map/psum | solution.py:45
  184.4 0.6 convert_divide_fusion
  185.1 8.2 %fusion.10 = f32[128,2048]{1,0:T(8,128)} fusion(bf16[2048,2432]{1,0:T(8,128)(2,1)} %bitcast.47, bf16[128,2432]{0,1:T(8,128)(2,1)S(1)} %copy.10, f32[2432,128]{1,0:T(8,128)S(1)} %get-tuple-element.162, f32[128]{0:T(128)S(1)} %log.7, f32[128]{0:T(128)S(1)} %pmax.7, f32[128]{0:T(128)S(1)} %log.6, f32[128]{0:T(128)S(1)} %get-tuple-element.137, ...), kind=kOutput, calls=%fused_computation.23 | convolution fusion | flops 1277558784 | bytes 12880384 | tf_op jit(solution)/shard_map/dot_general | solution.py:74
  193.3 0.0 copy-done.4
  193.3 0.0 reduce-scatter.2.cloned.1.call-update
  194.7 61.0 %reduce-scatter.2.cloned.1.call-done = f32[128,256]{1,0:T(8,128)} async-done(((f32[128,2048]{1,0:T(8,128)}), f32[128,256]{1,0:T(8,128)}) %reduce-scatter.2.cloned.1.call-update) | async-done | bytes 131088 | tf_op jit(solution)/shard_map/reduce_scatter | solution.py:77
  255.7 1.5 convert_element_type.16
  (12 shorter events, 0.2 us)
Async XLA Ops:
  7.2 107.5 %all-gather.6.cloned.1.call-start = ((), (), s32[]{:S(2)}) async-start(), calls=%async_computation.1 | async-start | bytes 12451840 | tf_op jit(solution)/shard_map/all_gather | solution.py:54
  10.1 30.5 %collective-permute-start = (bf16[256,2432]{1,0:T(8,128)(2,1)}, bf16[256,2432]{1,0:T(8,128)(2,1)S(1)}, u32[]{:S(2)}, u32[]{:S(2)}) collective-permute-start(bf16[256,2432]{1,0:T(8,128)(2,1)} %get-tuple-element.160), channel_id=1, source_target_pairs={{0,1},{1,0},{2,3},{3,2},{4,5},{5,4},{6,7},{7,6},{8,9},{9,8},{10,11... | collective-permute-start | bytes 3735560 | tf_op jit(solution)/shard_map/ppermute | solution.py:11
  42.5 1.1 copy-start
  42.5 213.1 %reduce-scatter.2.cloned.1.call-start = ((), (), s32[]{:S(2)}) async-start(), calls=%async_computation.2 | async-start | bytes 1179648 | tf_op jit(solution)/shard_map/reduce_scatter | solution.py:77
  43.6 39.9 %copy-start.1 = (bf16[128,256]{1,0:T(8,128)(2,1)S(1)}, bf16[128,256]{1,0:T(8,128)(2,1)}, u32[]{:S(2)}) copy-start(bf16[128,256]{1,0:T(8,128)(2,1)} %param.7) | copy-start | bytes 196612
  121.4 35.4 %copy-start.2 = (s32[128]{0:T(128)S(1)}, s32[128]{0:T(128)}, u32[]{:S(2)}) copy-start(s32[128]{0:T(128)} %param.10) | copy-start | bytes 1540
  121.7 55.9 %copy-start.3 = (s32[128]{0:T(128)S(1)}, s32[128]{0:T(128)}, u32[]{:S(2)}) copy-start(s32[128]{0:T(128)} %param.11) | copy-start | bytes 1540
  177.6 15.8 %copy-start.4 = (f32[128]{0:T(128)}, f32[128]{0:T(128)S(1)}, u32[]{:S(2)}) copy-start(f32[128]{0:T(128)S(1)} %get-tuple-element.153) | copy-start | bytes 1540
Sparse Core Ops, SparseCore 0:
  42.6 68.6 all-gather.5
  193.5 62.1 reduce-scatter.1
where the time goes:
time: 266 us; the launch traced here: 265 us
  blocking collectives  131 us (49%)
  waiting for transfers between devices  88.6 us (33%)
  between operations  16.6 us (6%)
  matrix products  14.9 us (6%)
  other arithmetic  6.81 us (3%)
  local copies, waits for them, and re-layouts  4.23 us (2%)
  starting transfers between devices  3.05 us (1%)
    reduce_scatter x1, waiting for transfers between devices, on_device(): lax.psum_scatter(term, 'vocab', scatter_dimension=1, tiled=True)  61 us
    all_gather x2, blocking collectives, combined_all(): gathered = jax.tree.map(lambda a: lax.all_gather(a, axis), part)  34.7 us
    all_gather x1, blocking collectives, on_device(): gathered = lax.all_gather(student_hidden, 'vocab', axis=1, tiled=True)  31.2 us
    ppermute x1, waiting for transfers between devices, swapped(): lax.ppermute(shard, axis, [(i, i ^ 1 << stride) for i in range(lax.axis_s...  27.6 us
    pmax x1, blocking collectives, on_device(): teacher_max = lax.pmax(jnp.max(teacher_full, axis=1), 'vocab')  21.9 us
    psum x1, blocking collectives, on_device(): token_kl, sampled = lax.psum((kl_part, sampled_part), 'vocab')  19.7 us
    psum x1, blocking collectives, on_device(): lax.psum(jnp.sum(jnp.exp(teacher_full - teacher_max[:, None]), axis=1), '...  17.1 us
    dot_general x1, matrix products, on_device(): lax.dot_general(dlogits, weight, (((1,), (1,)), ((), ())), preferred_elem...  8.22 us
  transfers between devices with their start and end apart: 3, of which 2 were waited for; matrix products, arithmetic and copies ran while one was open for 0% of the time, Pallas kernels for 0%

commit v1 on v0

--- a/solution.py
+++ b/solution.py
@@ -5,6 +5,13 @@
 
 D = 2048
 VT = 2432
+
+
+def swapped_in(x, axis, dim):
+    devices = lax.axis_size(axis)
+    parts = jnp.stack([x for _ in range(devices)])
+    parts = lax.all_to_all(parts, axis, split_axis=0, concat_axis=0)
+    return jnp.concatenate(parts, axis=dim)
 
 
 def swapped(shard, axis, stride):
@@ -43,7 +50,7 @@
     pair_side = vocab_index % 2
     mask_float = loss_mask.astype(jnp.float32)
     mask_total = lax.psum(jnp.sum(mask_float), "dp")
-    gathered = lax.all_gather(student_hidden, "vocab", axis=1, tiled=True)
+    gathered = swapped_in(student_hidden, "vocab", 1)
     piece = student_blocks[0]
     own_block = lax.dynamic_slice_in_dim(piece, pair_side * VT, VT, 1)
     far_block = lax.dynamic_slice_in_dim(piece, (1 - pair_side) * VT, VT, 1)

time: 266 us -> 263 us (0.989)
  blocking collectives: 131 us -> 104 us
  waiting for transfers between devices: 88.6 us -> 106 us
  starting transfers between devices: 3.05 us -> 9.1 us
    all_gather x1 -> x0, blocking collectives: 31.2 us -> none  [on_device(): gathered = lax.all_gather(student_hidden, 'vocab', axis=1, tiled=True)]
    all_gather x1, waiting for transfers between devices: 0.01 us -> 19.1 us  [on_device(): weight = lax.all_gather(stacked, 'dp', axis=1, tiled=True).reshape(D, VT)]
    all_to_all x0 -> x1, starting transfers between devices: none -> 6.06 us  [swapped_in(): parts = lax.all_to_all(parts, axis, split_axis=0, concat_axis=0)]
  transfers between devices with their start and end apart: 3 -> 4, of which waited for: 2 -> 3; matrix products, arithmetic and copies ran while one was open for 0% -> 1% of each run, Pallas kernels for 0% -> 0%
where the time goes in v1:
time: 263 us
  waiting for transfers between devices  106 us (40%)
  blocking collectives  104 us (40%)
  between operations  16.6 us (6%)
  matrix products  14.8 us (6%)
  starting transfers between devices  9.1 us (3%)
  other arithmetic  6.81 us (3%)
  local copies, waits for them, and re-layouts  5.05 us (2%)
    reduce_scatter x1, waiting for transfers between devices, on_device(): lax.psum_scatter(term, 'vocab', scatter_dimension=1, tiled=True)  59.5 us
    all_gather x2, blocking collectives, combined_all(): gathered = jax.tree.map(lambda a: lax.all_gather(a, axis), part)  36.9 us
    ppermute x1, waiting for transfers between devices, swapped(): lax.ppermute(shard, axis, [(i, i ^ 1 << stride) for i in range(lax.axis_s...  27.6 us
    pmax x1, blocking collectives, on_device(): teacher_max = lax.pmax(jnp.max(teacher_full, axis=1), 'vocab')  22.1 us
    psum x1, blocking collectives, on_device(): token_kl, sampled = lax.psum((kl_part, sampled_part), 'vocab')  19.7 us
    all_gather x1, waiting for transfers between devices, on_device(): weight = lax.all_gather(stacked, 'dp', axis=1, tiled=True).reshape(D, VT)  19.1 us
    psum x1, blocking collectives, on_device(): lax.psum(jnp.sum(jnp.exp(teacher_full - teacher_max[:, None]), axis=1), '...  18.9 us
    dot_general x1, matrix products, on_device(): lax.dot_general(dlogits, weight, (((1,), (1,)), ((), ())), preferred_elem...  8.2 us
  transfers between devices with their start and end apart: 4, of which 3 were waited for; matrix products, arithmetic and copies ran while one was open for 1% of the time, Pallas kernels for 0%

profile of v1, /device:TPU:0, one launch (start us, length us, event | category | flops | bytes accessed | tf_op | source)
XLA Modules:
  0.0 262.8 jit_solution(11672858103054976847)
XLA Ops:
  7.2 0.0 all-gather.6.cloned.1.call-start
  7.2 2.9 %constant_dynamic-slice_fusion.1 = (bf16[1,256,2432]{2,1,0:T(8,128)(2,1)S(1)}, bf16[256,2432]{1,0:T(8,128)(2,1)}) fusion(bf16[1,256,4864]{2,1,0:T(8,128)(2,1)} %param.8, s32[]{:T(128)S(6)} %select_n.41, s32[]{:T(128)S(6)} %select_n.42), kind=kLoop, calls=%fused_computation.33 | loop fusion | bytes 4980744 | tf_op jit(solution)/shard_map/dynamic_slice | solution.py:55
  10.1 3.0 %collective-permute-start = (bf16[256,2432]{1,0:T(8,128)(2,1)}, bf16[256,2432]{1,0:T(8,128)(2,1)S(1)}, u32[]{:S(2)}, u32[]{:S(2)}) collective-permute-start(bf16[256,2432]{1,0:T(8,128)(2,1)} %get-tuple-element.160), channel_id=1, source_target_pairs={{0,1},{1,0},{2,3},{3,2},{4,5},{5,4},{6,7},{7,6},{8,9},{9,8},{10,11... | collective-permute-start | bytes 3735560 | tf_op jit(solution)/shard_map/ppermute | solution.py:18
  13.1 27.6 %collective-permute-done = bf16[256,2432]{1,0:T(8,128)(2,1)S(1)} collective-permute-done((bf16[256,2432]{1,0:T(8,128)(2,1)}, bf16[256,2432]{1,0:T(8,128)(2,1)S(1)}, u32[]{:S(2)}, u32[]{:S(2)}) %collective-permute-start) | collective-permute-done | bytes 1245216 | tf_op jit(solution)/shard_map/ppermute | solution.py:18
  40.7 1.8 maximum_select_fusion
  42.5 0.0 copy-start.1
  42.5 0.0 all-gather.6.cloned.1.call-update
  42.5 0.8 copy-done.1
  43.3 0.0 copy-start
  43.3 0.1 copy.12
  43.5 0.9 stack.11
  44.3 6.1 %all-to-all-start = ((bf16[8,128,256]{1,2,0:T(8,128)(2,1)}), bf16[8,128,256]{1,2,0:T(8,128)(2,1)S(1)}, u32[]{:S(2)}, u32[]{:S(2)}) async-start(bf16[8,128,256]{1,2,0:T(8,128)(2,1)} %stack.11), calls=%async_computation | async-start | bytes 1048576 | tf_op jit(solution)/shard_map/all_to_all | solution.py:13
  50.4 0.0 reduce-scatter.2.cloned.1.call-start
  50.4 0.0 copy-done
  50.5 0.3 copy.13
  50.8 0.2 reduce_max.24
  51.0 22.1 %pmax.7 = f32[128]{0:T(128)S(1)} all-reduce(bf16[128]{0:T(256)(128)(2,1)S(1)} %reduce_max.24), channel_id=1, replica_groups=mesh['dp'=4,'vocab'=8] {'vocab'}, use_global_device_ids=true, to_apply=%region_7.8 | all-reduce | flops 128 | bytes 768 | tf_op jit(solution)/shard_map/pmax | solution.py:66
  73.1 0.3 exponential_reduce_fusion
  73.4 18.9 %psum.36 = f32[128]{0:T(128)S(1)} all-reduce(f32[128]{0:T(128)S(1)} %exponential_reduce_fusion), channel_id=1, replica_groups=mesh['dp'=4,'vocab'=8] {'vocab'}, use_global_device_ids=true, to_apply=%region_9.10 | all-reduce | flops 128 | bytes 1024 | tf_op jit(solution)/shard_map/psum | solution.py:67
  92.3 0.0 all-to-all-done
  92.3 19.1 %all-gather.6.cloned.1.call-done = bf16[2,1024,2432]{2,1,0:T(8,128)(2,1)} async-done(((bf16[2,256,2432]{2,1,0:T(8,128)(2,1)}), bf16[2,1024,2432]{2,1,0:T(8,128)(2,1)}) %all-gather.6.cloned.1.call-update) | async-done | bytes 9961488 | tf_op jit(solution)/shard_map/all_gather | solution.py:61
  111.4 6.6 %fusion.17 = (f32[128]{0:T(128)S(1)}, f32[2432,128]{1,0:T(8,128)S(1)}) fusion(bf16[2048,2432]{1,0:T(8,128)(2,1)} %bitcast.49, bf16[128,2048]{0,1:T(8,128)(2,1)S(1)} %bitcast.52), kind=kOutput, calls=%fused_computation.36 | convolution fusion | flops 1275379584 | bytes 11731456 | tf_op jit(solution)/shard_map/dot_general | solution.py:62
  118.0 0.0 copy-start.2
  118.0 0.3 exponential_reduce_fusion.1
  118.4 0.0 copy-start.3
  118.4 20.6 %all-gather.3 = f32[8,1,128]{2,1,0:T(1,128)S(1)} all-gather(f32[1,1,128]{2,1,0:T(1,128)S(1)} %bitcast.56), channel_id=3, replica_groups=mesh['dp'=4,'vocab'=8] {'vocab'}, dimensions={0}, use_global_device_ids=true | all-gather | bytes 4608 | tf_op jit(solution)/shard_map/all_gather | solution.py:22
  139.0 16.3 %all-gather.2 = f32[8,1,128]{2,1,0:T(1,128)S(1)} all-gather(f32[1,1,128]{2,1,0:T(1,128)S(1)} %bitcast.55), channel_id=2, replica_groups=mesh['dp'=4,'vocab'=8] {'vocab'}, dimensions={0}, use_global_device_ids=true | all-gather | bytes 4608 | tf_op jit(solution)/shard_map/all_gather | solution.py:22
  155.3 0.3 while.17
  155.6 0.0 copy-done.2
  155.6 1.1 fusion.7
  156.7 19.7 %all-reduce = (f32[128]{0:T(128)S(1)}, f32[128]{0:T(128)}) all-reduce(f32[128]{0:T(128)S(1)} %get-tuple-element.140, f32[128]{0:T(128)S(1)} %get-tuple-element.139), channel_id=1, replica_groups=mesh['dp'=4,'vocab'=8] {'vocab'}, use_global_device_ids=true, to_apply=%region_12.13 | all-reduce | flops 256 | bytes 2048 | tf_op jit(solution)/shard_map/psum | solution.py:77
  176.4 0.0 copy-start.4
  176.4 0.0 copy-done.3
  176.4 0.6 multiply_reduce_fusion
  177.0 6.5 %all-reduce.1 = (f32[]{:T(128)}, f32[]{:T(128)}) all-reduce(f32[]{:T(128)} %get-tuple-element.142, f32[]{:T(128)} %get-tuple-element.141), channel_id=1, replica_groups=mesh['dp'=4,'vocab'=8] {'dp'}, use_global_device_ids=true, to_apply=%region_1.2 | all-reduce | flops 2 | bytes 16 | tf_op jit(solution)/shard_map/psum | solution.py:52
  183.6 0.6 convert_divide_fusion
  184.2 8.2 %fusion.10 = f32[128,2048]{1,0:T(8,128)} fusion(bf16[2048,2432]{1,0:T(8,128)(2,1)} %bitcast.50, bf16[128,2432]{0,1:T(8,128)(2,1)S(1)} %copy.13, f32[2432,128]{1,0:T(8,128)S(1)} %get-tuple-element.162, f32[128]{0:T(128)S(1)} %log.7, f32[128]{0:T(128)S(1)} %pmax.7, f32[128]{0:T(128)S(1)} %log.6, f32[128]{0:T(128)S(1)} %get-tuple-element.137, ...), kind=kOutput, calls=%fused_computation.23 | convolution fusion | flops 1277558784 | bytes 12880384 | tf_op jit(solution)/shard_map/dot_general | solution.py:81
  192.4 0.0 copy-done.4
  192.4 0.0 reduce-scatter.2.cloned.1.call-update
  193.8 59.5 %reduce-scatter.2.cloned.1.call-done = f32[128,256]{1,0:T(8,128)} async-done(((f32[128,2048]{1,0:T(8,128)}), f32[128,256]{1,0:T(8,128)}) %reduce-scatter.2.cloned.1.call-update) | async-done | bytes 131088 | tf_op jit(solution)/shard_map/reduce_scatter | solution.py:84
  253.3 1.5 convert_element_type.16
  (12 shorter events, 0.2 us)
Async XLA Ops:
  7.2 104.2 %all-gather.6.cloned.1.call-start = ((), (), s32[]{:S(2)}) async-start(), calls=%async_computation.2 | async-start | bytes 12451840 | tf_op jit(solution)/shard_map/all_gather | solution.py:61
  10.1 30.5 %collective-permute-start = (bf16[256,2432]{1,0:T(8,128)(2,1)}, bf16[256,2432]{1,0:T(8,128)(2,1)S(1)}, u32[]{:S(2)}, u32[]{:S(2)}) collective-permute-start(bf16[256,2432]{1,0:T(8,128)(2,1)} %get-tuple-element.160), channel_id=1, source_target_pairs={{0,1},{1,0},{2,3},{3,2},{4,5},{5,4},{6,7},{7,6},{8,9},{9,8},{10,11... | collective-permute-start | bytes 3735560 | tf_op jit(solution)/shard_map/ppermute | solution.py:18
  42.5 0.8 copy-start.1
  43.3 7.1 %copy-start = (bf16[128,2432]{1,0:T(8,128)(2,1)S(1)}, bf16[128,2432]{1,0:T(8,128)(2,1)}, u32[]{:S(2)}) copy-start(bf16[128,2432]{1,0:T(8,128)(2,1)} %param.9) | copy-start | bytes 1867780
  44.3 48.0 %all-to-all-start = ((bf16[8,128,256]{1,2,0:T(8,128)(2,1)}), bf16[8,128,256]{1,2,0:T(8,128)(2,1)S(1)}, u32[]{:S(2)}, u32[]{:S(2)}) async-start(bf16[8,128,256]{1,2,0:T(8,128)(2,1)} %stack.11), calls=%async_computation | async-start | bytes 1048576 | tf_op jit(solution)/shard_map/all_to_all | solution.py:13
  50.4 202.9 %reduce-scatter.2.cloned.1.call-start = ((), (), s32[]{:S(2)}) async-start(), calls=%async_computation.3 | async-start | bytes 1179648 | tf_op jit(solution)/shard_map/reduce_scatter | solution.py:84
  118.0 37.6 %copy-start.2 = (s32[128]{0:T(128)S(1)}, s32[128]{0:T(128)}, u32[]{:S(2)}) copy-start(s32[128]{0:T(128)} %param.10) | copy-start | bytes 1540
  118.4 58.0 %copy-start.3 = (s32[128]{0:T(128)S(1)}, s32[128]{0:T(128)}, u32[]{:S(2)}) copy-start(s32[128]{0:T(128)} %param.11) | copy-start | bytes 1540
  176.4 16.0 %copy-start.4 = (f32[128]{0:T(128)}, f32[128]{0:T(128)S(1)}, u32[]{:S(2)}) copy-start(f32[128]{0:T(128)S(1)} %get-tuple-element.153) | copy-start | bytes 1540
Sparse Core Ops, SparseCore 0:
  42.6 68.7 all-gather.5
  192.6 60.6 reduce-scatter.1
